TPU v7x, 32 devices: a whole 2x2x4 slice. The times are simulated.
32 devices in a mesh: groups: 2 (over y), row: 4 (over z), col: 4 (over x, core).
Axes of the slice: x: 2, y: 2, z: 4, core: 2. Of those that a mesh axis runs over, the one named last changes fastest.
Arguments:
- factors: float32 [8, 1280, 5120], P('groups', 'row', 'col'), parts along dimension 0, may hold values from -1.5 to 1.5, as said below
- right_side: float32 [8, 1280, 96], P(('groups', 'col'), 'row'), parts along dimension 0, may hold values from -6 to 6
Outputs:
- forward: float32 [8, 1280, 96], P(('groups', 'col'), 'row'), parts along dimension 0
- solution: float32 [8, 1280, 96], P(('groups', 'col'), 'row'), parts along dimension 0
There are 2 independent parts, one for each index of `groups`. A program takes and returns all parts, laid end to end along the dimension named above; each array names one. Nothing has to cross between parts.
Inputs may be any that keep to these rules, and one draw needn't show every extreme that they name: `factors`: off the diagonal tiles, the entries are those of L below and of U above. Diagonal tile k holds, strictly below its diagonal, the strictly lower part of the inverse of L's unit lower triangular diagonal tile, and on and above its diagonal the inverse of U's upper triangular diagonal tile.
All inputs are finite; a program needn't handle non-finite values.
Results may differ from a plain program's by a relative error of at most 0.00014.
Values sent between devices are 32-bit elements; how exact they have to be, the bound alone decides.
A program may use at most 128 MiB of HBM per device.

v0:
```python
import functools

import jax
import jax.numpy as jnp
from jax import lax
from jax.experimental import pallas as pl
from jax.experimental.pallas import tpu as pltpu
from jax.sharding import PartitionSpec as P

MESH = pl.DeviceIdType.MESH
CHUNKS = 4


def kernel(
    n_row, n_col, chunks, rows, size, width, window, depth,
    factors_hbm, rs_ref,
    fwd_ref, sol_ref,
    raw, ahi, alo, rs_pad, out_pad, rs_buf, v_buf, f_buf, w_buf, s_buf, t_buf, tb_buf, rin, rout, rbin, rbout,
    a_sem, v_send, v_recv, f_send, f_recv, w_send, w_recv, s_send, s_recv,
    r_send, r_recv, rb_send, rb_recv, b0_send,
):
    r = lax.axis_index("row")
    c = lax.axis_index("col")
    last = n_col - 1
    start = r * rows
    shift = pl.multiple_of(start % 128, 8)

    def load(k):
        dst = raw.at[k, pl.ds(shift, rows), pl.ds(0, size)]
        return pltpu.make_async_copy(factors_hbm.at[k], dst, a_sem.at[k])

    def start_load(i, _):
        load(lax.rem(c + i, n_col)).start()
        return 0

    lax.fori_loop(0, n_col, start_load, 0)

    barrier = pltpu.get_barrier_semaphore()

    def greet(i, _):
        rr, cc = i // n_col, i % n_col

        @pl.when(i != r * n_col + c)
        def _():
            pl.semaphore_signal(barrier, inc=1, device_id={"row": rr, "col": cc}, device_id_type=MESH)

        return 0

    lax.fori_loop(0, n_row * n_col, greet, 0)
    pl.semaphore_wait(barrier, n_row * n_col - 1)

    def remote(src, dst, send, recv, row, col):
        return pltpu.make_async_remote_copy(
            src_ref=src, dst_ref=dst, send_sem=send, recv_sem=recv,
            device_id={"row": row, "col": col}, device_id_type=MESH,
        )

    def around(d):
        half = (d + 1) // 2
        odd = d % 2
        return lax.rem(r + odd * half - (1 - odd) * half + n_row, n_row)

    def each_chunk(body):
        def step(q, _):
            body(q)
            return 0

        lax.fori_loop(0, chunks, step, 0)

    def each_row(body, first=0):
        def step(d, _):
            body(around(d))
            return 0

        lax.fori_loop(first, n_row, step, 0, unroll=n_row <= 4)

    def part(x, k, s):
        columns = pl.ds(pl.multiple_of((s * rows) // 128 * 128, 128), window)
        hi = x.astype(jnp.bfloat16)
        lo = (x - hi.astype(jnp.float32)).astype(jnp.bfloat16)
        both = jnp.concatenate([hi, lo], axis=0)
        dims = (((1,), (1,)), ((), ()))
        m = x.shape[0]
        one = lax.dot_general(both, ahi[k, :, columns], dims, preferred_element_type=jnp.float32)
        two = lax.dot_general(hi, alo[k, :, columns], dims, preferred_element_type=jnp.float32)
        return one[:m] + one[m:] + two

    def combine(buf, k, q, wait):
        def step(d, acc):
            s = around(d)
            if wait is not None:
                wait(q, s)
            return acc + part(buf[q, s], k, s)

        zero = jnp.zeros(buf.shape[2:], jnp.float32)
        return lax.fori_loop(0, n_row, step, zero, unroll=n_row <= 4)

    def arrival(buf, recv):
        def wait(q, s):
            remote(buf.at[q, s], buf.at[q, s], recv.at[q, s], recv.at[q, s], r, c).wait_recv()

        return wait

    def arrival_but_own(buf, recv):
        inner = arrival(buf, recv)

        def wait(q, s):
            @pl.when(s != r)
            def _():
                inner(q, s)

        return wait

    def to_row(src, buf, send, recv, q, row):
        return remote(src, buf.at[q, r], send.at[q, row], recv.at[q, r], row, c)

    portion = width // chunks
    rs_pad[...] = jnp.zeros(rs_pad.shape, jnp.float32)
    rs_pad[pl.ds(shift, rows), :width] = rs_ref[0]
    turned = rs_pad[...].T
    for q in range(chunks):
        rs_buf[q] = turned[q * portion : (q + 1) * portion]

    def deliver(buf, out_ref):
        whole = jnp.concatenate([buf[q, r] for q in range(chunks)], axis=0)
        spare = out_pad.shape[1] - width
        if spare:
            whole = jnp.concatenate([whole, jnp.zeros((spare, window), jnp.float32)], axis=0)
        out_pad[...] = whole.T
        out_ref[0] = out_pad[pl.ds(shift, rows), :width]

    @pl.when(c == 0)
    def _():
        def one(q):
            v_buf[q, r] = rs_buf[q]
            each_row(lambda row: to_row(rs_buf.at[q], v_buf, v_send, v_recv, q, row).start(), 1)

        each_chunk(one)

    def first_run(q):
        return remote(rs_buf.at[q], rin.at[c, q], r_send.at[c, q], r_recv.at[c, q], r, 0)

    @pl.when(c > 0)
    def _():
        each_chunk(lambda q: first_run(q).start())

    block = 16

    def split(src, dst, kind):
        def step(i, _):
            base = pl.multiple_of(i * block, block)
            line = lax.broadcasted_iota(jnp.int32, (block, depth), 0) + (base - shift)
            place = lax.broadcasted_iota(jnp.int32, (block, depth), 1)
            value = raw[src, pl.ds(base, block), :]
            keep = (line >= 0) & (line < rows) & (place < size)
            if kind == 1:
                value = jnp.where(place == line + start, 1.0, value)
                keep = keep & (place <= line + start)
            if kind == 2:
                keep = keep & (place >= line + start)
            value = jnp.where(keep, value, 0.0)
            hi = value.astype(jnp.bfloat16)
            ahi[dst, pl.ds(base, block), :] = hi
            alo[dst, pl.ds(base, block), :] = (value - hi.astype(jnp.float32)).astype(jnp.bfloat16)
            return 0

        lax.fori_loop(0, window // block, step, 0)

    def split_others():
        def step(i, _):
            k = lax.rem(c + i, n_col)
            load(k).wait()
            split(k, k, 0)
            return 0

        lax.fori_loop(1, n_col, step, 0)
        split(c, n_col, 2)

    load(c).wait()
    split(c, c, 1)

    @pl.when(c > 0)
    def _():
        split_others()

    def back_run(q):
        return remote(f_buf.at[q, r], rbin.at[c, q], b0_send.at[q], rb_recv.at[c, q], r, last)

    def solve_forward(wait):
        def one(q):
            acc = combine(v_buf, c, q, wait)
            f_buf[q, r] = acc
            each_row(lambda row: to_row(f_buf.at[q, r], f_buf, f_send, f_recv, q, row).start(), 1)

            @pl.when(c < last)
            def _():
                back_run(q).start()

        each_chunk(one)

    @pl.when(c == 0)
    def _():
        solve_forward(arrival_but_own(v_buf, v_recv))

    @pl.when(c > 0)
    def _():
        solve_forward(arrival(v_buf, v_recv))

    deliver(f_buf, fwd_ref)

    @pl.when(c == 0)
    def _():
        split_others()

    def wait_run(run, recv, k, q):
        remote(run.at[k, q], run.at[k, q], recv.at[k, q], recv.at[k, q], r, c).wait_recv()

    def sweep(buf, recv, first, count, step, run_in, run_recv, run_out, run_send, stage, out, send, out_recv):
        nxt = c + step
        wait = arrival_but_own(buf, recv)

        def one(q):
            acc = combine(buf, first, q, wait)
            wait_run(run_in, run_recv, first, q)
            stage[q] = run_in[first, q] - acc
            each_row(
                lambda row: remote(stage.at[q], out.at[q, r], send.at[q, row], out_recv.at[q, r], row, nxt).start()
            )

        each_chunk(one)

        def other(i, _):
            k = first + step * i

            def inner(q):
                acc = combine(buf, k, q, None)
                wait_run(run_in, run_recv, k, q)
                run_out[k, q] = run_in[k, q] - acc
                remote(run_out.at[k, q], run_in.at[k, q], run_send.at[k, q], run_recv.at[k, q], r, nxt).start()

            each_chunk(inner)
            return 0

        lax.fori_loop(1, count, other, 0)

    @pl.when(c < last)
    def _():
        sweep(f_buf, f_recv, c + 1, last - c, 1, rin, r_recv, rout, r_send, t_buf, v_buf, w_send, v_recv)


    def solve_backward(buf, wait):
        def one(q):
            acc = combine(buf, n_col, q, wait)
            s_buf[q, r] = acc

            @pl.when(c > 0)
            def _():
                each_row(lambda row: to_row(s_buf.at[q, r], s_buf, s_send, s_recv, q, row).start(), 1)


        each_chunk(one)

    @pl.when(c == last)
    def _():
        solve_backward(f_buf, arrival_but_own(f_buf, f_recv))

    @pl.when(c < last)
    def _():
        solve_backward(w_buf, arrival(w_buf, w_recv))

    @pl.when(c > 0)
    def _():
        sweep(s_buf, s_recv, c - 1, c, -1, rbin, rb_recv, rbout, rb_send, tb_buf, w_buf, v_send, w_recv)

    deliver(s_buf, sol_ref)

    def sent(src, send):
        remote(src, src, send, send, r, c).wait_send()

    def finish(q):
        @pl.when(c == 0)
        def _():
            each_row(lambda row: sent(rs_buf.at[q], v_send.at[q, row]), 1)

        @pl.when(c > 0)
        def _():
            sent(rs_buf.at[q], r_send.at[c, q])
            each_row(lambda row: sent(tb_buf.at[q], v_send.at[q, row]))
            each_row(lambda row: sent(s_buf.at[q, r], s_send.at[q, row]), 1)

        each_row(lambda row: sent(f_buf.at[q, r], f_send.at[q, row]), 1)

        @pl.when(c < last)
        def _():
            sent(f_buf.at[q, r], b0_send.at[q])
            each_row(lambda row: sent(t_buf.at[q], w_send.at[q, row]))

        def run(k, _):
            @pl.when(k > c + 1)
            def _():
                sent(rout.at[k, q], r_send.at[k, q])

            @pl.when(k < c - 1)
            def _():
                sent(rbout.at[k, q], rb_send.at[k, q])

            return 0

        lax.fori_loop(0, n_col, run, 0)

    each_chunk(finish)


def local(n_row, n_col, factors, right_side):
    tiles, rows, size = factors.shape
    width = right_side.shape[2]
    chunks = CHUNKS
    portion = width // chunks
    starts = [i * rows for i in range(n_row)]
    window = max(-(-(i % 128 + rows) // 128) * 128 for i in starts)
    depth = max(max(i // 128 * 128 + window for i in starts), size)
    lanes = -(-width // 128) * 128

    vmem = pl.BlockSpec(memory_space=pltpu.VMEM)
    anywhere = pl.BlockSpec(memory_space=pl.ANY)
    gathered = pltpu.VMEM((chunks, n_row, portion, window), jnp.float32)
    staged = pltpu.VMEM((chunks, portion, window), jnp.float32)
    runs = pltpu.VMEM((tiles, chunks, portion, window), jnp.float32)
    weights = pltpu.VMEM((tiles + 1, window, depth), jnp.bfloat16)
    turning = pltpu.VMEM((window, lanes), jnp.float32)
    dma = pltpu.SemaphoreType.DMA
    shape = jax.ShapeDtypeStruct(right_side.shape, jnp.float32)
    return pl.pallas_call(
        functools.partial(kernel, n_row, n_col, chunks, rows, size, width, window, depth),
        out_shape=(shape, shape),
        in_specs=[anywhere, vmem],
        out_specs=(vmem, vmem),
        scratch_shapes=[
            pltpu.VMEM((tiles, window, depth), jnp.float32), weights, weights, turning, turning, staged,
            gathered, gathered, gathered, gathered, staged, staged, runs, runs, runs, runs,
            dma((tiles,)),
            *([dma((chunks, n_row))] * 8),
            *([dma((tiles, chunks))] * 4),
            dma((chunks,)),
        ],
        compiler_params=pltpu.CompilerParams(collective_id=0, has_side_effects=True, vmem_limit_bytes=60 << 20),
    )(factors, right_side)


def solution(mesh):
    return jax.shard_map(
        functools.partial(local, mesh.shape["row"], mesh.shape["col"]),
        mesh=mesh,
        in_specs=(P("groups", "row", "col"), P(("groups", "col"), "row", None)),
        out_specs=(P(("groups", "col"), "row", None), P(("groups", "col"), "row", None)),
        check_vma=False,
    )
```

profile of v0, /device:TPU:0, one launch (start us, length us, event | category | flops | bytes accessed | tf_op | source)
XLA Modules:
  0.0 107.6 jit_solution(11284034681446316924)
XLA Ops:
  0.6 1.7 %copy.4.rs_ref = f32[1,320,96]{2,1,0:T(8,128)} copy(f32[1,320,96]{1,2,0:T(8,128)} %param.3) | data formatting | bytes 245760 | tf_op args[1]
  2.3 101.9 %shard_map.41 = (f32[1,320,96]{2,1,0:T(8,128)}, f32[1,320,96]{2,1,0:T(8,128)}) custom-call(f32[4,320,1280]{2,1,0:T(8,128)} %factors_hbm.1, f32[1,320,96]{2,1,0:T(8,128)} %copy.4.rs_ref), custom_call_target="tpu_custom_call" | custom-call | tf_op jit(solution)/shard_map/pallas_call | solution.py:333
  104.2 1.7 %copy.5 = f32[1,320,96]{1,2,0:T(8,128)} copy(f32[1,320,96]{2,1,0:T(8,128)} %get-tuple-element.2) | data formatting | bytes 245760 | tf_op jit(solution)/shard_map/pallas_call | solution.py:333
  105.9 1.7 %copy.6 = f32[1,320,96]{1,2,0:T(8,128)} copy(f32[1,320,96]{2,1,0:T(8,128)} %get-tuple-element.3) | data formatting | bytes 245760 | tf_op jit(solution)/shard_map/pallas_call | solution.py:333
where the time goes:
time: 108 us
  Pallas kernels  102 us (94%)
  local copies, waits for them, and re-layouts  5.09 us (5%)
    pallas_call x1, Pallas kernels, local(): pl.pallas_call(functools.partial(kernel, n_row, n_col, chunks, rows, size...  102 us
    pallas_call x2, local copies, waits for them, and re-layouts, local(): pl.pallas_call(functools.partial(kernel, n_row, n_col, chunks, rows, size...  3.4 us

commit v1 on v0

v1 whole, which is shorter than its diff:
```python
import functools

import jax
import jax.numpy as jnp
from jax import lax
from jax.experimental import pallas as pl
from jax.experimental.pallas import tpu as pltpu
from jax.sharding import PartitionSpec as P

MESH = pl.DeviceIdType.MESH
CHUNKS = 6
TURN = 256


def kernel(
    n_row, n_col, chunks, rows, size, width,
    factors_hbm, rs_ref,
    fwd_ref, sol_ref,
    raw, turned, corner, ahi, alo, v_buf, f_buf, w_buf, s_buf, t_buf, tb_buf, rin, rout, rbin, rbout,
    a_sem, v_send, v_recv, f_send, f_recv, w_send, w_recv, s_send, s_recv,
    r_send, r_recv, rb_send, rb_recv, b0_send,
):
    r = lax.axis_index("row")
    c = lax.axis_index("col")
    last = n_col - 1
    portion = width // chunks
    short = n_row <= 4

    def load(k):
        return pltpu.make_async_copy(factors_hbm.at[k], raw.at[k, pl.ds(0, rows), :], a_sem.at[k])

    def start_load(i, _):
        load(lax.rem(c + i, n_col)).start()
        return 0

    lax.fori_loop(0, n_col, start_load, 0)

    barrier = pltpu.get_barrier_semaphore()

    def greet(i, _):
        rr, cc = i // n_col, i % n_col

        @pl.when(i != r * n_col + c)
        def _():
            pl.semaphore_signal(barrier, inc=1, device_id={"row": rr, "col": cc}, device_id_type=MESH)

        return 0

    lax.fori_loop(0, n_row * n_col, greet, 0)
    pl.semaphore_wait(barrier, n_row * n_col - 1)

    def remote(src, dst, send, recv, row, col):
        return pltpu.make_async_remote_copy(
            src_ref=src, dst_ref=dst, send_sem=send, recv_sem=recv,
            device_id={"row": row, "col": col}, device_id_type=MESH,
        )

    def each_chunk(body):
        def step(q, _):
            body(q)
            return 0

        lax.fori_loop(0, chunks, step, 0)

    def each_row(body):
        def step(s, _):
            body(s)
            return 0

        lax.fori_loop(0, n_row, step, 0, unroll=short)

    def far_first(body, up, down, own):
        def step(i, _):
            d = n_row - 1 - i
            if up:
                @pl.when(r + d < n_row)
                def _():
                    body(r + d)

            if down:
                @pl.when(r - d >= 0)
                def _():
                    body(r - d)

            return 0

        lax.fori_loop(0, n_row - 1, step, 0, unroll=short)
        if own:
            body(r)

    def split(x):
        hi = x.astype(jnp.bfloat16)
        return hi, (x - hi.astype(jnp.float32)).astype(jnp.bfloat16)

    def combine(buf, k, q):
        def step(s, acc):
            hi, lo = split(buf[q, s])
            both = jnp.concatenate([hi, lo], axis=0)
            one = jnp.dot(both, ahi[k, s], preferred_element_type=jnp.float32)
            two = jnp.dot(hi, alo[k, s], preferred_element_type=jnp.float32)
            return acc + (one[:portion] + one[portion:] + two)

        zero = jnp.zeros((portion, rows), jnp.float32)
        return lax.fori_loop(0, n_row, step, zero, unroll=short)

    def arrive(buf, recv, q, s):
        remote(buf.at[q, s], buf.at[q, s], recv.at[q, s], recv.at[q, s], r, c).wait_recv()

    def arrivals(buf, recv, q, up, down, own):
        def one(s):
            wanted = None if own else s != r
            if not up:
                wanted = s <= r if own else s < r
            if not down:
                wanted = s >= r if own else s > r
            if wanted is None:
                arrive(buf, recv, q, s)
            else:
                @pl.when(wanted)
                def _():
                    arrive(buf, recv, q, s)

        each_row(one)

    def chunk(ref, q):
        return ref.at[0, pl.ds(pl.multiple_of(q * portion, 8), portion), :]

    def to_row(src, buf, send, recv, q, row, col):
        return remote(src, buf.at[q, r], send.at[q, row], recv.at[q, r], row, col)

    @pl.when(c == 0)
    def _():
        def one(q):
            far_first(lambda row: to_row(chunk(rs_ref, q), v_buf, v_send, v_recv, q, row, c).start(), True, False, False)
            v_buf[q, r] = chunk(rs_ref, q)[...]

        each_chunk(one)

    def first_run(q):
        return remote(chunk(rs_ref, q), rin.at[c, q], r_send.at[c, q], r_recv.at[c, q], r, 0)

    @pl.when(c > 0)
    def _():
        each_chunk(lambda q: first_run(q).start())

    def blank(s):
        zero = jnp.zeros((chunks, portion, rows), jnp.float32)

        @pl.when(s > r)
        def _():
            v_buf[:, s] = zero

        @pl.when(s < r)
        def _():
            w_buf[:, s] = zero

            @pl.when(c == last)
            def _():
                f_buf[:, s] = zero

    each_row(blank)

    def turn(k):
        def step(j, _):
            base = pl.multiple_of(j * TURN, TURN)
            turned[pl.ds(base, TURN), :] = raw[k, :, pl.ds(base, TURN)].T
            return 0

        load(k).wait()
        lax.fori_loop(0, size // TURN, step, 0)

        def cut(s, _):
            hi, lo = split(turned[pl.ds(pl.multiple_of(s * rows, 8), rows), :rows])
            ahi[k, s] = hi
            alo[k, s] = lo
            return 0

        lax.fori_loop(0, n_row, cut, 0)

    def place():
        return lax.broadcasted_iota(jnp.int32, (rows, rows), 0), lax.broadcasted_iota(jnp.int32, (rows, rows), 1)

    def set_lower():
        column, line = place()
        value = turned[pl.ds(pl.multiple_of(r * rows, 8), rows), :rows]
        corner[...] = value
        value = jnp.where(column < line, value, jnp.where(column == line, 1.0, 0.0))
        ahi[c, r], alo[c, r] = split(value)

    def set_upper():
        column, line = place()
        ahi[c, r], alo[c, r] = split(jnp.where(column >= line, corner[...], 0.0))

    turn(c)
    set_lower()

    @pl.when(c == 0)
    def _():
        turn(c + 1)

    @pl.when(c > 0)
    def _():
        def step(i, _):
            turn(lax.rem(c + i, n_col))
            return 0

        lax.fori_loop(1, n_col, step, 0)

    def back_run(q):
        return remote(f_buf.at[q, r], rbin.at[c, q], b0_send.at[q], rb_recv.at[c, q], r, last)

    def deliver(ref, q, value):
        ref[0, pl.ds(pl.multiple_of(q * portion, 8), portion), :] = value

    def solve_forward(own):
        def one(q):
            arrivals(v_buf, v_recv, q, False, True, own)
            acc = combine(v_buf, c, q)
            f_buf[q, r] = acc

            @pl.when(c < last)
            def _():
                far_first(lambda row: to_row(f_buf.at[q, r], f_buf, f_send, f_recv, q, row, c).start(), True, True, False)
                back_run(q).start()

            @pl.when(c == last)
            def _():
                far_first(lambda row: to_row(f_buf.at[q, r], f_buf, f_send, f_recv, q, row, c).start(), False, True, False)

            deliver(fwd_ref, q, acc)

        each_chunk(one)

    @pl.when(c == 0)
    def _():
        solve_forward(False)

    @pl.when(c > 0)
    def _():
        solve_forward(True)

    def wait_run(run, recv, k, q):
        remote(run.at[k, q], run.at[k, q], recv.at[k, q], recv.at[k, q], r, c).wait_recv()

    def sweep(buf, recv, first, count, step, run_in, run_recv, run_out, run_send, stage, out, send, out_recv, late):
        nxt = c + step

        def one(q):
            arrivals(buf, recv, q, True, True, False)
            acc = combine(buf, first, q)
            wait_run(run_in, run_recv, first, q)
            stage[q] = run_in[first, q] - acc
            far_first(
                lambda row: to_row(stage.at[q], out, send, out_recv, q, row, nxt).start(),
                step > 0, step < 0, True,
            )

        each_chunk(one)

        def other(i, _):
            k = first + step * i
            if late:
                @pl.when(c == 0)
                def _():
                    turn(k)

            def inner(q):
                acc = combine(buf, k, q)
                wait_run(run_in, run_recv, k, q)
                run_out[k, q] = run_in[k, q] - acc
                remote(run_out.at[k, q], run_in.at[k, q], run_send.at[k, q], run_recv.at[k, q], r, nxt).start()

            each_chunk(inner)
            return 0

        lax.fori_loop(1, count, other, 0)

    @pl.when(c == last)
    def _():
        set_upper()

    @pl.when(c < last)
    def _():
        sweep(f_buf, f_recv, c + 1, last - c, 1, rin, r_recv, rout, r_send, t_buf, v_buf, w_send, v_recv, True)
        set_upper()

    def solve_backward(buf, recv, own):
        def one(q):
            arrivals(buf, recv, q, True, False, own)
            acc = combine(buf, c, q)

            @pl.when(c > 0)
            def _():
                s_buf[q, r] = acc
                far_first(lambda row: to_row(s_buf.at[q, r], s_buf, s_send, s_recv, q, row, c).start(), True, True, False)

            deliver(sol_ref, q, acc)

        each_chunk(one)

    @pl.when(c == last)
    def _():
        solve_backward(f_buf, f_recv, False)

    @pl.when(c < last)
    def _():
        solve_backward(w_buf, w_recv, True)

    @pl.when(c > 0)
    def _():
        sweep(s_buf, s_recv, c - 1, c, -1, rbin, rb_recv, rbout, rb_send, tb_buf, w_buf, v_send, w_recv, False)

    def sent(src, send):
        remote(src, src, send, send, r, c).wait_send()

    def finish(q):
        @pl.when(c == 0)
        def _():
            far_first(lambda row: sent(chunk(rs_ref, q), v_send.at[q, row]), True, False, False)

        @pl.when(c > 0)
        def _():
            sent(chunk(rs_ref, q), r_send.at[c, q])
            far_first(lambda row: sent(tb_buf.at[q], v_send.at[q, row]), False, True, True)
            far_first(lambda row: sent(s_buf.at[q, r], s_send.at[q, row]), True, True, False)

        @pl.when(c < last)
        def _():
            far_first(lambda row: sent(f_buf.at[q, r], f_send.at[q, row]), True, True, False)
            sent(f_buf.at[q, r], b0_send.at[q])
            far_first(lambda row: sent(t_buf.at[q], w_send.at[q, row]), True, False, True)

        @pl.when(c == last)
        def _():
            far_first(lambda row: sent(f_buf.at[q, r], f_send.at[q, row]), False, True, False)

        def run(k, _):
            @pl.when(k > c + 1)
            def _():
                sent(rout.at[k, q], r_send.at[k, q])

            @pl.when(k < c - 1)
            def _():
                sent(rbout.at[k, q], rb_send.at[k, q])

            return 0

        lax.fori_loop(0, n_col, run, 0)

    each_chunk(finish)


def local(n_row, n_col, factors, right_side):
    tiles, rows, size = factors.shape
    width = right_side.shape[2]
    chunks = CHUNKS
    portion = width // chunks
    padded = -(-rows // 128) * 128

    vmem = pl.BlockSpec(memory_space=pltpu.VMEM)
    anywhere = pl.BlockSpec(memory_space=pl.ANY)
    gathered = pltpu.VMEM((chunks, n_row, portion, rows), jnp.float32)
    staged = pltpu.VMEM((chunks, portion, rows), jnp.float32)
    runs = pltpu.VMEM((tiles, chunks, portion, rows), jnp.float32)
    weights = pltpu.VMEM((tiles, n_row, rows, rows), jnp.bfloat16)
    dma = pltpu.SemaphoreType.DMA
    shape = jax.ShapeDtypeStruct((1, width, rows), jnp.float32)
    forward, backward = pl.pallas_call(
        functools.partial(kernel, n_row, n_col, chunks, rows, size, width),
        out_shape=(shape, shape),
        in_specs=[anywhere, vmem],
        out_specs=(vmem, vmem),
        scratch_shapes=[
            pltpu.VMEM((tiles, padded, size), jnp.float32), pltpu.VMEM((size, padded), jnp.float32),
            pltpu.VMEM((rows, rows), jnp.float32), weights, weights,
            gathered, gathered, gathered, gathered, staged, staged, runs, runs, runs, runs,
            dma((tiles,)),
            *([dma((chunks, n_row))] * 8),
            *([dma((tiles, chunks))] * 4),
            dma((chunks,)),
        ],
        compiler_params=pltpu.CompilerParams(collective_id=0, has_side_effects=True, vmem_limit_bytes=60 << 20),
    )(factors, right_side.transpose(0, 2, 1))
    return forward.transpose(0, 2, 1), backward.transpose(0, 2, 1)


def solution(mesh):
    return jax.shard_map(
        functools.partial(local, mesh.shape["row"], mesh.shape["col"]),
        mesh=mesh,
        in_specs=(P("groups", "row", "col"), P(("groups", "col"), "row", None)),
        out_specs=(P(("groups", "col"), "row", None), P(("groups", "col"), "row", None)),
        check_vma=False,
    )
```

time: 108 us -> 104 us (0.963)
  Pallas kernels: 102 us -> 99.7 us
  local copies, waits for them, and re-layouts: 5.09 us -> 3.16 us
    pallas_call x2 -> x0, local copies, waits for them, and re-layouts: 3.4 us -> none  [local(): pl.pallas_call(functools.partial(kernel, n_row, n_col, chunks, rows, size...]
    pallas_call x1, Pallas kernels: 102 us -> 99.7 us  [local(): pl.pallas_call(functools.partial(kernel, n_row, n_col, chunks, rows, size...]
    unnamed x1 -> x2, local copies, waits for them, and re-layouts: 1.69 us -> 3.16 us
where the time goes in v1:
time: 104 us; the launch traced here: 103 us
  Pallas kernels  99.7 us (96%)
  local copies, waits for them, and re-layouts  3.16 us (3%)
    pallas_call x1, Pallas kernels, local(): pl.pallas_call(functools.partial(kernel, n_row, n_col, chunks, rows, size...  99.7 us
    unnamed x2, local copies, waits for them, and re-layouts  3.16 us

profile of v1, /device:TPU:0, one launch (start us, length us, event | category | flops | bytes accessed | tf_op | source)
XLA Modules:
  0.0 103.5 jit_solution(6064153808808553787)
XLA Ops:
  0.6 99.7 %shard_map.41 = (f32[1,96,320]{2,1,0:T(8,128)}, f32[1,96,320]{2,1,0:T(8,128)}) custom-call(f32[4,320,1280]{2,1,0:T(8,128)} %factors_hbm.1, f32[1,96,320]{2,1,0:T(8,128)} %bitcast.3), custom_call_target="tpu_custom_call" | custom-call | tf_op jit(solution)/shard_map/pallas_call | solution.py:368
  100.3 1.6 %copy.6 = f32[1,320,96]{1,2,0:T(8,128)} copy(f32[1,320,96]{1,2,0:T(8,128)} %bitcast.5) | data formatting | bytes 245760
  101.9 1.6 %copy.7 = f32[1,320,96]{1,2,0:T(8,128)} copy(f32[1,320,96]{1,2,0:T(8,128)} %bitcast.4) | data formatting | bytes 245760

commit v2 on v1

v2 whole, which is shorter than its diff:
```python
import functools

import jax
import jax.numpy as jnp
from jax import lax
from jax.experimental import pallas as pl
from jax.experimental.pallas import tpu as pltpu
from jax.sharding import PartitionSpec as P

MESH = pl.DeviceIdType.MESH
CHUNKS = 6
TURN = 256
LAG = 1


def kernel(
    n_row, n_col, chunks, rows, size, width, spare,
    factors_hbm, rs_ref,
    fwd_ref, sol_ref,
    raw, turned, ahi, alo, rs_buf, v_buf, f_buf, w_buf, s_buf, t_buf, tb_buf, rin, rout, rbin, rbout,
    a_sem, v_send, v_recv, f_send, f_recv, w_send, w_recv, s_send, s_recv,
    r_send, r_recv, rb_send, rb_recv, b0_send,
):
    r = lax.axis_index("row")
    c = lax.axis_index("col")
    last = n_col - 1
    portion = width // chunks
    short = n_row <= 4
    depth = rows + spare
    whole = rows // 128

    def load(k):
        return pltpu.make_async_copy(factors_hbm.at[k], raw.at[k, pl.ds(0, rows), :], a_sem.at[k, 0])

    def load_spare(k):
        src = factors_hbm.at[k, pl.ds(rows - spare, spare), :]
        return pltpu.make_async_copy(src, raw.at[k, pl.ds(rows, spare), :], a_sem.at[k, 1])

    def start_load(i, _):
        load(lax.rem(c + i, n_col)).start()
        if spare:
            load_spare(lax.rem(c + i, n_col)).start()
        return 0

    lax.fori_loop(0, n_col, start_load, 0)

    barrier = pltpu.get_barrier_semaphore()

    def greet(i, _):
        rr, cc = i // n_col, i % n_col

        @pl.when(i != r * n_col + c)
        def _():
            pl.semaphore_signal(barrier, inc=1, device_id={"row": rr, "col": cc}, device_id_type=MESH)

        return 0

    lax.fori_loop(0, n_row * n_col, greet, 0)

    def remote(src, dst, send, recv, row, col):
        return pltpu.make_async_remote_copy(
            src_ref=src, dst_ref=dst, send_sem=send, recv_sem=recv,
            device_id={"row": row, "col": col}, device_id_type=MESH,
        )

    def each_chunk(body):
        def step(q, _):
            body(q)
            return 0

        lax.fori_loop(0, chunks, step, 0)

    def each_row(body):
        def step(s, _):
            body(s)
            return 0

        lax.fori_loop(0, n_row, step, 0, unroll=short)

    def far_first(body, up, down, own):
        def step(i, _):
            d = n_row - 1 - i
            if up:
                @pl.when(r + d < n_row)
                def _():
                    body(r + d)

            if down:
                @pl.when(r - d >= 0)
                def _():
                    body(r - d)

            return 0

        lax.fori_loop(0, n_row - 1, step, 0, unroll=short)
        if own:
            body(r)

    def split(x):
        hi = x.astype(jnp.bfloat16)
        return hi, (x - hi.astype(jnp.float32)).astype(jnp.bfloat16)

    def halves(value):
        lane = lax.broadcasted_iota(jnp.int32, value.shape, 1)
        return lane < spare

    def unpack(block):
        if not spare:
            return block
        parts = [block[i * portion : (i + 1) * portion] for i in range(whole)]
        rest = block[whole * portion :]
        left = halves(rest)
        parts.append(jnp.concatenate([jnp.where(left, rest, 0.0), jnp.where(left, 0.0, rest)], axis=0))
        return jnp.concatenate(parts, axis=1)

    def pack(value):
        if not spare:
            return value
        parts = [value[:, i * 128 : (i + 1) * 128] for i in range(whole)]
        rest = value[:, whole * 128 :]
        top, low = rest[: portion // 2], rest[portion // 2 :]
        return jnp.concatenate([*parts, jnp.where(halves(top), top, low)], axis=0)

    def combine(buf, index, q):
        def step(s, acc):
            hi, lo = split(unpack(buf[q, s]))
            both = jnp.concatenate([hi, lo], axis=0)
            one = jnp.dot(both, ahi[index(s)], preferred_element_type=jnp.float32)
            two = jnp.dot(hi, alo[index(s)], preferred_element_type=jnp.float32)
            return acc + (one[:portion] + one[portion:] + two)

        zero = jnp.zeros((portion, depth), jnp.float32)
        return lax.fori_loop(0, n_row, step, zero, unroll=short)

    def tile(k):
        return lambda s: k * n_row + s

    def upper(s):
        same = 1 // (1 + (s - r) * (s - r))
        return c * n_row + s + same * ((n_col - c) * n_row - s)

    def arrive(buf, recv, q, s):
        remote(buf.at[q, s], buf.at[q, s], recv.at[q, s], recv.at[q, s], r, c).wait_recv()

    def arrivals(buf, recv, q, up, down, own):
        def one(s):
            wanted = None if own else s != r
            if not up:
                wanted = s <= r if own else s < r
            if not down:
                wanted = s >= r if own else s > r
            if wanted is None:
                arrive(buf, recv, q, s)
            else:
                @pl.when(wanted)
                def _():
                    arrive(buf, recv, q, s)

        each_row(one)

    def to_row(src, buf, send, recv, q, row, col):
        return remote(src, buf.at[q, r], send.at[q, row], recv.at[q, r], row, col)

    def prepare(q):
        value = rs_ref[0, pl.ds(pl.multiple_of(q * portion, 8), portion), :]
        if spare:
            value = jnp.concatenate([value, value[:, rows - spare :]], axis=1)
        rs_buf[q] = pack(value)

        @pl.when(c == 0)
        def _():
            v_buf[q, r] = rs_buf[q]

    each_chunk(prepare)

    def blank(s):
        zero = jnp.zeros((chunks, *v_buf.shape[2:]), jnp.float32)

        @pl.when(s > r)
        def _():
            v_buf[:, s] = zero

        @pl.when(s < r)
        def _():
            w_buf[:, s] = zero

            @pl.when(c == last)
            def _():
                f_buf[:, s] = zero

    each_row(blank)

    def store(at, value):
        hi, lo = split(value)
        ahi[at, pl.ds(0, rows), :] = hi
        alo[at, pl.ds(0, rows), :] = lo
        if spare:
            ahi[at, pl.ds(rows, spare), :] = hi[rows - spare :]
            alo[at, pl.ds(rows, spare), :] = lo[rows - spare :]

    def band(s):
        return turned[pl.ds(pl.multiple_of(s * rows, 8), rows), :depth]

    def turn(k):
        def step(j, _):
            base = pl.multiple_of(j * TURN, TURN)
            turned[pl.ds(base, TURN), :] = raw[k, :, pl.ds(base, TURN)].T
            return 0

        load(k).wait()
        if spare:
            load_spare(k).wait()
        lax.fori_loop(0, size // TURN, step, 0)

        def cut(s, _):
            store(k * n_row + s, band(s))
            return 0

        lax.fori_loop(0, n_row, cut, 0)

    def corners():
        column = lax.broadcasted_iota(jnp.int32, (rows, depth), 0)
        line = lax.broadcasted_iota(jnp.int32, (rows, depth), 1)
        line = line - jnp.where(line >= rows, spare, 0)
        value = band(r)
        store(c * n_row + r, jnp.where(column < line, value, jnp.where(column == line, 1.0, 0.0)))
        store(n_col * n_row, jnp.where(column >= line, value, 0.0))

    turn(c)
    corners()
    pl.semaphore_wait(barrier, n_row * n_col - 1)

    @pl.when(c == 0)
    def _():
        def one(q):
            far_first(lambda row: to_row(rs_buf.at[q], v_buf, v_send, v_recv, q, row, c).start(), True, False, False)

        each_chunk(one)

    def first_run(q):
        return remote(rs_buf.at[q], rin.at[c, q], r_send.at[c, q], r_recv.at[c, q], r, 0)

    @pl.when(c > 0)
    def _():
        each_chunk(lambda q: first_run(q).start())

    def turn_others(i, _):
        turn(lax.rem(c + i, n_col))
        return 0

    lax.fori_loop(1, n_col, turn_others, 0)

    def back_run(q):
        return remote(f_buf.at[q, r], rbin.at[c, q], b0_send.at[q], rb_recv.at[c, q], r, last)

    def deliver(ref, q, value):
        ref[0, pl.ds(pl.multiple_of(q * portion, 8), portion), :] = value[:, :rows]

    def forward_of(own, is_last):
        def one(q):
            arrivals(v_buf, v_recv, q, False, True, own)
            acc = combine(v_buf, tile(c), q)
            f_buf[q, r] = pack(acc)
            far_first(
                lambda row: to_row(f_buf.at[q, r], f_buf, f_send, f_recv, q, row, c).start(), not is_last, True, False
            )
            if not is_last:
                back_run(q).start()
            deliver(fwd_ref, q, acc)

        return one

    def wait_run(run, recv, k, q):
        remote(run.at[k, q], run.at[k, q], recv.at[k, q], recv.at[k, q], r, c).wait_recv()

    def sweep_of(buf, recv, count, step, run_in, run_recv, run_out, run_send, stage, out, send, out_recv):
        nxt = c + step

        def one(q):
            arrivals(buf, recv, q, True, True, False)
            acc = combine(buf, tile(nxt), q)
            wait_run(run_in, run_recv, nxt, q)
            stage[q] = run_in[nxt, q] - pack(acc)
            far_first(
                lambda row: to_row(stage.at[q], out, send, out_recv, q, row, nxt).start(),
                step > 0, step < 0, True,
            )

            def other(i, _):
                k = nxt + step * i
                acc = combine(buf, tile(k), q)
                wait_run(run_in, run_recv, k, q)
                run_out[k, q] = run_in[k, q] - pack(acc)
                remote(run_out.at[k, q], run_in.at[k, q], run_send.at[k, q], run_recv.at[k, q], r, nxt).start()
                return 0

            lax.fori_loop(1, count, other, 0)

        return one

    def backward_of(buf, recv, own, is_first):
        def one(q):
            arrivals(buf, recv, q, True, False, own)
            acc = combine(buf, upper, q)
            if not is_first:
                s_buf[q, r] = pack(acc)
                far_first(lambda row: to_row(s_buf.at[q, r], s_buf, s_send, s_recv, q, row, c).start(), True, True, False)
            deliver(sol_ref, q, acc)

        return one

    def pipeline(*bodies):
        def step(t, _):
            for i, body in enumerate(bodies):
                @pl.when((t >= i * LAG) & (t < i * LAG + chunks))
                def _():
                    body(t - i * LAG)

            return 0

        lax.fori_loop(0, chunks + (len(bodies) - 1) * LAG, step, 0)

    down = sweep_of(f_buf, f_recv, last - c, 1, rin, r_recv, rout, r_send, t_buf, v_buf, w_send, v_recv)
    back = sweep_of(s_buf, s_recv, c, -1, rbin, rb_recv, rbout, rb_send, tb_buf, w_buf, v_send, w_recv)

    @pl.when(c == 0)
    def _():
        pipeline(forward_of(False, False), down)
        pipeline(backward_of(w_buf, w_recv, True, True))

    @pl.when((c > 0) & (c < last))
    def _():
        pipeline(forward_of(True, False), down)
        pipeline(backward_of(w_buf, w_recv, True, False), back)

    @pl.when(c == last)
    def _():
        pipeline(forward_of(True, True), backward_of(f_buf, f_recv, False, False), back)

    def sent(src, send):
        remote(src, src, send, send, r, c).wait_send()

    def finish(q):
        @pl.when(c == 0)
        def _():
            far_first(lambda row: sent(rs_buf.at[q], v_send.at[q, row]), True, False, False)

        @pl.when(c > 0)
        def _():
            sent(rs_buf.at[q], r_send.at[c, q])
            far_first(lambda row: sent(tb_buf.at[q], v_send.at[q, row]), False, True, True)
            far_first(lambda row: sent(s_buf.at[q, r], s_send.at[q, row]), True, True, False)

        @pl.when(c < last)
        def _():
            far_first(lambda row: sent(f_buf.at[q, r], f_send.at[q, row]), True, True, False)
            sent(f_buf.at[q, r], b0_send.at[q])
            far_first(lambda row: sent(t_buf.at[q], w_send.at[q, row]), True, False, True)

        @pl.when(c == last)
        def _():
            far_first(lambda row: sent(f_buf.at[q, r], f_send.at[q, row]), False, True, False)

        def run(k, _):
            @pl.when(k > c + 1)
            def _():
                sent(rout.at[k, q], r_send.at[k, q])

            @pl.when(k < c - 1)
            def _():
                sent(rbout.at[k, q], rb_send.at[k, q])

            return 0

        lax.fori_loop(0, n_col, run, 0)

    each_chunk(finish)


def local(n_row, n_col, factors, right_side):
    tiles, rows, size = factors.shape
    width = right_side.shape[2]
    chunks = CHUNKS
    portion = width // chunks
    spare = 64 if rows % 128 == 64 and portion % 16 == 0 else 0
    padded = -(-rows // 128) * 128
    depth = rows + spare

    vmem = pl.BlockSpec(memory_space=pltpu.VMEM)
    anywhere = pl.BlockSpec(memory_space=pl.ANY)
    block = (portion * depth // 128 - spare * portion // 128, 128) if spare else (portion, rows)
    gathered = pltpu.VMEM((chunks, n_row, *block), jnp.float32)
    staged = pltpu.VMEM((chunks, *block), jnp.float32)
    runs = pltpu.VMEM((tiles, chunks, *block), jnp.float32)
    weights = pltpu.VMEM((tiles * n_row + 1, depth, depth), jnp.bfloat16)
    dma = pltpu.SemaphoreType.DMA
    shape = jax.ShapeDtypeStruct((1, width, rows), jnp.float32)
    forward, backward = pl.pallas_call(
        functools.partial(kernel, n_row, n_col, chunks, rows, size, width, spare),
        out_shape=(shape, shape),
        in_specs=[anywhere, vmem],
        out_specs=(vmem, vmem),
        scratch_shapes=[
            pltpu.VMEM((tiles, padded, size), jnp.float32), pltpu.VMEM((size, padded), jnp.float32),
            weights, weights, staged,
            gathered, gathered, gathered, gathered, staged, staged, runs, runs, runs, runs,
            dma((tiles, 2)),
            *([dma((chunks, n_row))] * 8),
            *([dma((tiles, chunks))] * 4),
            dma((chunks,)),
        ],
        compiler_params=pltpu.CompilerParams(collective_id=0, has_side_effects=True, vmem_limit_bytes=60 << 20),
    )(factors, right_side.transpose(0, 2, 1))
    return forward.transpose(0, 2, 1), backward.transpose(0, 2, 1)


def solution(mesh):
    return jax.shard_map(
        functools.partial(local, mesh.shape["row"], mesh.shape["col"]),
        mesh=mesh,
        in_specs=(P("groups", "row", "col"), P(("groups", "col"), "row", None)),
        out_specs=(P(("groups", "col"), "row", None), P(("groups", "col"), "row", None)),
        check_vma=False,
    )
```

time: 104 us -> 90.6 us (0.87)
  Pallas kernels: 99.7 us -> 86.7 us
    pallas_call x1, Pallas kernels: 99.7 us -> 86.7 us  [local(): pl.pallas_call(functools.partial(kernel, n_row, n_col, chunks, rows, size...]
where the time goes in v2:
time: 90.6 us; the launch traced here: 90.5 us
  Pallas kernels  86.7 us (96%)
  local copies, waits for them, and re-layouts  3.16 us (3%)
    pallas_call x1, Pallas kernels, local(): pl.pallas_call(functools.partial(kernel, n_row, n_col, chunks, rows, size...  86.7 us
    unnamed x2, local copies, waits for them, and re-layouts  3.16 us

profile of v2, /device:TPU:0, one launch (start us, length us, event | category | flops | bytes accessed | tf_op | source)
XLA Modules:
  0.0 90.5 jit_solution(6770252657736830338)
XLA Ops:
  0.6 86.7 %shard_map.41 = (f32[1,96,320]{2,1,0:T(8,128)}, f32[1,96,320]{2,1,0:T(8,128)}) custom-call(f32[4,320,1280]{2,1,0:T(8,128)} %factors_hbm.1, f32[1,96,320]{2,1,0:T(8,128)} %bitcast.3), custom_call_target="tpu_custom_call" | custom-call | tf_op jit(solution)/shard_map/pallas_call | solution.py:398
  87.3 1.6 %copy.6 = f32[1,320,96]{1,2,0:T(8,128)} copy(f32[1,320,96]{1,2,0:T(8,128)} %bitcast.5) | data formatting | bytes 245760
  88.9 1.6 %copy.7 = f32[1,320,96]{1,2,0:T(8,128)} copy(f32[1,320,96]{1,2,0:T(8,128)} %bitcast.4) | data formatting | bytes 245760

commit v3 on v2

--- a/solution.py
+++ b/solution.py
@@ -10,7 +10,8 @@
 MESH = pl.DeviceIdType.MESH
 CHUNKS = 6
 TURN = 256
-LAG = 1
+GROUPS = 2
+DELAY = 3
 
 
 def kernel(
@@ -19,7 +20,7 @@
     fwd_ref, sol_ref,
     raw, turned, ahi, alo, rs_buf, v_buf, f_buf, w_buf, s_buf, t_buf, tb_buf, rin, rout, rbin, rbout,
     a_sem, v_send, v_recv, f_send, f_recv, w_send, w_recv, s_send, s_recv,
-    r_send, r_recv, rb_send, rb_recv, b0_send,
+    r_send, r_recv, rb_send, rb_recv, b0_send, g_send,
 ):
     r = lax.axis_index("row")
     c = lax.axis_index("col")
@@ -77,24 +78,64 @@
 
         lax.fori_loop(0, n_row, step, 0, unroll=short)
 
-    def far_first(body, up, down, own):
+    def far_first(body, up, down, own, top=None, bottom=None):
         def step(i, _):
             d = n_row - 1 - i
+            if down:
+                @pl.when(r - d >= (0 if bottom is None else bottom))
+                def _():
+                    body(r - d)
+
             if up:
-                @pl.when(r + d < n_row)
+                @pl.when(r + d <= (n_row - 1 if top is None else top))
                 def _():
                     body(r + d)
-
-            if down:
-                @pl.when(r - d >= 0)
-                def _():
-                    body(r - d)
 
             return 0
 
         lax.fori_loop(0, n_row - 1, step, 0, unroll=short)
         if own:
             body(r)
+
+    relays = g_send.shape[1] > 1
+    half = n_row // 2
+    mirror = n_row - 1 - half
+
+    def spread(body, ahead):
+        if not relays:
+            far_first(body, True, True, False)
+        elif ahead:
+            @pl.when(r < half)
+            def _():
+                far_first(body, True, True, False, top=half)
+
+            @pl.when(r >= half)
+            def _():
+                far_first(body, True, True, False)
+        else:
+            @pl.when(r > mirror)
+            def _():
+                far_first(body, True, True, False, bottom=mirror)
+
+            @pl.when(r <= mirror)
+            def _():
+                far_first(body, True, True, False)
+
+    def relayed(body, ahead):
+        if not relays:
+            return
+        if ahead:
+            @pl.when(r == half)
+            def _():
+                for s in range(half):
+                    for row in range(half + 1, n_row):
+                        body(s, row, row - half - 1)
+        else:
+            @pl.when(r == mirror)
+            def _():
+                for s in range(n_row - 1, mirror, -1):
+                    for row in range(mirror):
+                        body(s, row, row)
 
     def split(x):
         hi = x.astype(jnp.bfloat16)
@@ -121,9 +162,11 @@
         top, low = rest[: portion // 2], rest[portion // 2 :]
         return jnp.concatenate([*parts, jnp.where(halves(top), top, low)], axis=0)
 
-    def combine(buf, index, q):
+    def combine(buf, index, q, count=1):
+        portion = width // chunks * count
+
         def step(s, acc):
-            hi, lo = split(unpack(buf[q, s]))
+            hi, lo = split(jnp.concatenate([unpack(buf[q + i, s]) for i in range(count)], axis=0))
             both = jnp.concatenate([hi, lo], axis=0)
             one = jnp.dot(both, ahi[index(s)], preferred_element_type=jnp.float32)
             two = jnp.dot(hi, alo[index(s)], preferred_element_type=jnp.float32)
@@ -158,6 +201,35 @@
 
         each_row(one)
 
+    def gather(buf, recv, q, ahead):
+        def one(i):
+            s = i if ahead else n_row - 1 - i
+            wanted = s != r
+            if relays and ahead:
+                wanted = wanted & ((r != half) | (s > half))
+            if relays and not ahead:
+                wanted = wanted & ((r != mirror) | (s < mirror))
+
+            @pl.when(wanted)
+            def _():
+                arrive(buf, recv, q, s)
+
+        each_row(one)
+
+    def relay(buf, recv, q, s, row, slot):
+        return remote(buf.at[q, s], buf.at[q, s], g_send.at[q, s, slot], recv.at[q, s], row, c)
+
+    def pass_on_of(buf, recv, ahead):
+        def one(q):
+            def step(s, row, slot):
+                if slot == 0:
+                    arrive(buf, recv, q, s)
+                relay(buf, recv, q, s, row, slot).start()
+
+            relayed(step, ahead)
+
+        return one
+
     def to_row(src, buf, send, recv, q, row, col):
         return remote(src, buf.at[q, r], send.at[q, row], recv.at[q, r], row, col)
 
@@ -230,12 +302,19 @@
     corners()
     pl.semaphore_wait(barrier, n_row * n_col - 1)
 
+    def enter(q):
+        far_first(lambda row: to_row(rs_buf.at[q], v_buf, v_send, v_recv, q, row, c).start(), True, False, False)
+
+    def each_of(g, body):
+        def step(i, _):
+            body(g * (chunks // GROUPS) + i)
+            return 0
+
+        lax.fori_loop(0, chunks // GROUPS, step, 0)
+
     @pl.when(c == 0)
     def _():
-        def one(q):
-            far_first(lambda row: to_row(rs_buf.at[q], v_buf, v_send, v_recv, q, row, c).start(), True, False, False)
-
-        each_chunk(one)
+        each_of(0, enter)
 
     def first_run(q):
         return remote(rs_buf.at[q], rin.at[c, q], r_send.at[c, q], r_recv.at[c, q], r, 0)
@@ -261,10 +340,10 @@
             arrivals(v_buf, v_recv, q, False, True, own)
             acc = combine(v_buf, tile(c), q)
             f_buf[q, r] = pack(acc)
-            far_first(
-                lambda row: to_row(f_buf.at[q, r], f_buf, f_send, f_recv, q, row, c).start(), not is_last, True, False
-            )
-            if not is_last:
+            if is_last:
+                far_first(lambda row: to_row(f_buf.at[q, r], f_buf, f_send, f_recv, q, row, c).start(), False, True, False)
+            else:
+                spread(lambda row: to_row(f_buf.at[q, r], f_buf, f_send, f_recv, q, row, c).start(), True)
                 back_run(q).start()
             deliver(fwd_ref, q, acc)
 
@@ -277,7 +356,7 @@
         nxt = c + step
 
         def one(q):
-            arrivals(buf, recv, q, True, True, False)
+            gather(buf, recv, q, step > 0)
             acc = combine(buf, tile(nxt), q)
             wait_run(run_in, run_recv, nxt, q)
             stage[q] = run_in[nxt, q] - pack(acc)
@@ -286,17 +365,22 @@
                 step > 0, step < 0, True,
             )
 
+        def rest(g):
+            each = chunks // GROUPS
+
             def other(i, _):
                 k = nxt + step * i
-                acc = combine(buf, tile(k), q)
-                wait_run(run_in, run_recv, k, q)
-                run_out[k, q] = run_in[k, q] - pack(acc)
-                remote(run_out.at[k, q], run_in.at[k, q], run_send.at[k, q], run_recv.at[k, q], r, nxt).start()
+                acc = combine(buf, tile(k), g * each, each)
+                for part in range(each):
+                    q = g * each + part
+                    wait_run(run_in, run_recv, k, q)
+                    run_out[k, q] = run_in[k, q] - pack(acc[part * portion : (part + 1) * portion])
+                    remote(run_out.at[k, q], run_in.at[k, q], run_send.at[k, q], run_recv.at[k, q], r, nxt).start()
                 return 0
 
             lax.fori_loop(1, count, other, 0)
 
-        return one
+        return one, rest
 
     def backward_of(buf, recv, own, is_first):
         def one(q):
@@ -304,38 +388,61 @@
             acc = combine(buf, upper, q)
             if not is_first:
                 s_buf[q, r] = pack(acc)
-                far_first(lambda row: to_row(s_buf.at[q, r], s_buf, s_send, s_recv, q, row, c).start(), True, True, False)
+                spread(lambda row: to_row(s_buf.at[q, r], s_buf, s_send, s_recv, q, row, c).start(), False)
             deliver(sol_ref, q, acc)
 
         return one
 
-    def pipeline(*bodies):
+    def pipeline(final, *stages):
         def step(t, _):
-            for i, body in enumerate(bodies):
-                @pl.when((t >= i * LAG) & (t < i * LAG + chunks))
+            for first, body in stages:
+                @pl.when((t >= first) & (t < first + DELAY * GROUPS) & ((t + DELAY - first % DELAY) % DELAY == 0))
                 def _():
-                    body(t - i * LAG)
-
-            return 0
-
-        lax.fori_loop(0, chunks + (len(bodies) - 1) * LAG, step, 0)
-
-    down = sweep_of(f_buf, f_recv, last - c, 1, rin, r_recv, rout, r_send, t_buf, v_buf, w_send, v_recv)
-    back = sweep_of(s_buf, s_recv, c, -1, rbin, rb_recv, rbout, rb_send, tb_buf, w_buf, v_send, w_recv)
+                    if body in (down_rest, back_rest):
+                        body((t - first) // DELAY)
+                    else:
+                        each_of((t - first) // DELAY, body)
+
+            return 0
+
+        lax.fori_loop(0, final + DELAY * (GROUPS - 1) + 1, step, 0)
+
+    down, down_rest = sweep_of(f_buf, f_recv, last - c, 1, rin, r_recv, rout, r_send, t_buf, v_buf, w_send, v_recv)
+    back, back_rest = sweep_of(s_buf, s_recv, c, -1, rbin, rb_recv, rbout, rb_send, tb_buf, w_buf, v_send, w_recv)
+
+    pass_down = pass_on_of(f_buf, f_recv, True)
+    pass_back = pass_on_of(s_buf, s_recv, False)
 
     @pl.when(c == 0)
     def _():
-        pipeline(forward_of(False, False), down)
-        pipeline(backward_of(w_buf, w_recv, True, True))
+        def enter_next(q):
+            @pl.when(q + chunks // GROUPS < chunks)
+            def _():
+                enter(q + chunks // GROUPS)
+
+        pipeline(
+            4 * last + 1,
+            (1, pass_down), (1, down), (0, forward_of(False, False)), (DELAY - 1, enter_next), (1, down_rest),
+            (4 * last + 1, backward_of(w_buf, w_recv, True, True)),
+        )
 
     @pl.when((c > 0) & (c < last))
     def _():
-        pipeline(forward_of(True, False), down)
-        pipeline(backward_of(w_buf, w_recv, True, False), back)
+        turned_back = 4 * (last - c) + 1
+        pipeline(
+            turned_back + 1,
+            (turned_back + 1, pass_back), (turned_back + 1, back), (turned_back, backward_of(w_buf, w_recv, True, False)),
+            (1, pass_down), (1, down), (0, forward_of(True, False)),
+            (1, down_rest), (turned_back + 1, back_rest),
+        )
 
     @pl.when(c == last)
     def _():
-        pipeline(forward_of(True, True), backward_of(f_buf, f_recv, False, False), back)
+        pipeline(
+            2,
+            (2, pass_back), (2, back), (1, backward_of(f_buf, f_recv, False, False)), (0, forward_of(True, True)),
+            (2, back_rest),
+        )
 
     def sent(src, send):
         remote(src, src, send, send, r, c).wait_send()
@@ -349,11 +456,13 @@
         def _():
             sent(rs_buf.at[q], r_send.at[c, q])
             far_first(lambda row: sent(tb_buf.at[q], v_send.at[q, row]), False, True, True)
-            far_first(lambda row: sent(s_buf.at[q, r], s_send.at[q, row]), True, True, False)
+            spread(lambda row: sent(s_buf.at[q, r], s_send.at[q, row]), False)
+            relayed(lambda s, row, slot: sent(s_buf.at[q, s], g_send.at[q, s, slot]), False)
 
         @pl.when(c < last)
         def _():
-            far_first(lambda row: sent(f_buf.at[q, r], f_send.at[q, row]), True, True, False)
+            spread(lambda row: sent(f_buf.at[q, r], f_send.at[q, row]), True)
+            relayed(lambda s, row, slot: sent(f_buf.at[q, s], g_send.at[q, s, slot]), True)
             sent(f_buf.at[q, r], b0_send.at[q])
             far_first(lambda row: sent(t_buf.at[q], w_send.at[q, row]), True, False, True)
 
@@ -407,7 +516,7 @@
             dma((tiles, 2)),
             *([dma((chunks, n_row))] * 8),
             *([dma((tiles, chunks))] * 4),
-            dma((chunks,)),
+            dma((chunks,)), dma((chunks, n_row, n_row // 2) if 2 < n_row <= 8 else (1, 1, 1)),
         ],
         compiler_params=pltpu.CompilerParams(collective_id=0, has_side_effects=True, vmem_limit_bytes=60 << 20),
     )(factors, right_side.transpose(0, 2, 1))

time: 90.6 us -> 88.2 us (0.974)
  Pallas kernels: 86.7 us -> 84.2 us
    pallas_call x1, Pallas kernels: 86.7 us -> 84.2 us  [local(): pl.pallas_call(functools.partial(kernel, n_row, n_col, chunks, rows, size...]
where the time goes in v3:
time: 88.2 us; the launch traced here: 88 us
  Pallas kernels  84.2 us (95%)
  local copies, waits for them, and re-layouts  3.16 us (4%)
    pallas_call x1, Pallas kernels, local(): pl.pallas_call(functools.partial(kernel, n_row, n_col, chunks, rows, size...  84.2 us
    unnamed x2, local copies, waits for them, and re-layouts  3.16 us

profile of v3, /device:TPU:0, one launch (start us, length us, event | category | flops | bytes accessed | tf_op | source)
XLA Modules:
  0.0 88.0 jit_solution(18292300963404422887)
XLA Ops:
  0.6 84.2 %shard_map.41 = (f32[1,96,320]{2,1,0:T(8,128)}, f32[1,96,320]{2,1,0:T(8,128)}) custom-call(f32[4,320,1280]{2,1,0:T(8,128)} %factors_hbm.1, f32[1,96,320]{2,1,0:T(8,128)} %bitcast.3), custom_call_target="tpu_custom_call" | custom-call | tf_op jit(solution)/shard_map/pallas_call | solution.py:507
  84.8 1.6 %copy.6 = f32[1,320,96]{1,2,0:T(8,128)} copy(f32[1,320,96]{1,2,0:T(8,128)} %bitcast.5) | data formatting | bytes 245760
  86.4 1.6 %copy.7 = f32[1,320,96]{1,2,0:T(8,128)} copy(f32[1,320,96]{1,2,0:T(8,128)} %bitcast.4) | data formatting | bytes 245760

commit v4 on v3

--- a/solution.py
+++ b/solution.py
@@ -71,12 +71,12 @@
 
         lax.fori_loop(0, chunks, step, 0)
 
-    def each_row(body):
+    def each_row(body, first=0, stop=n_row):
         def step(s, _):
             body(s)
             return 0
 
-        lax.fori_loop(0, n_row, step, 0, unroll=short)
+        lax.fori_loop(first, stop, step, 0, unroll=short)
 
     def far_first(body, up, down, own, top=None, bottom=None):
         def step(i, _):
@@ -162,7 +162,7 @@
         top, low = rest[: portion // 2], rest[portion // 2 :]
         return jnp.concatenate([*parts, jnp.where(halves(top), top, low)], axis=0)
 
-    def combine(buf, index, q, count=1):
+    def combine(buf, index, q, count=1, first=0, stop=n_row, start=None):
         portion = width // chunks * count
 
         def step(s, acc):
@@ -172,8 +172,17 @@
             two = jnp.dot(hi, alo[index(s)], preferred_element_type=jnp.float32)
             return acc + (one[:portion] + one[portion:] + two)
 
-        zero = jnp.zeros((portion, depth), jnp.float32)
-        return lax.fori_loop(0, n_row, step, zero, unroll=short)
+        if start is None:
+            start = jnp.zeros((portion, depth), jnp.float32)
+        return lax.fori_loop(first, stop, step, start, unroll=short)
+
+    def combine_as_they_come(buf, index, q, wait, last_row):
+        others = (1, n_row) if last_row == 0 else (0, n_row - 1)
+        final = (last_row, last_row + 1)
+        wait(*others)
+        acc = combine(buf, index, q, 1, *others)
+        wait(*final)
+        return combine(buf, index, q, 1, *final, acc)
 
     def tile(k):
         return lambda s: k * n_row + s
@@ -185,7 +194,7 @@
     def arrive(buf, recv, q, s):
         remote(buf.at[q, s], buf.at[q, s], recv.at[q, s], recv.at[q, s], r, c).wait_recv()
 
-    def arrivals(buf, recv, q, up, down, own):
+    def arrivals(buf, recv, q, up, down, own, first, stop):
         def one(s):
             wanted = None if own else s != r
             if not up:
@@ -199,11 +208,11 @@
                 def _():
                     arrive(buf, recv, q, s)
 
-        each_row(one)
-
-    def gather(buf, recv, q, ahead):
+        each_row(one, first, stop)
+
+    def gather(buf, recv, q, ahead, first, stop):
         def one(i):
-            s = i if ahead else n_row - 1 - i
+            s = i if ahead else first + stop - 1 - i
             wanted = s != r
             if relays and ahead:
                 wanted = wanted & ((r != half) | (s > half))
@@ -214,7 +223,7 @@
             def _():
                 arrive(buf, recv, q, s)
 
-        each_row(one)
+        each_row(one, first, stop)
 
     def relay(buf, recv, q, s, row, slot):
         return remote(buf.at[q, s], buf.at[q, s], g_send.at[q, s, slot], recv.at[q, s], row, c)
@@ -337,8 +346,8 @@
 
     def forward_of(own, is_last):
         def one(q):
-            arrivals(v_buf, v_recv, q, False, True, own)
-            acc = combine(v_buf, tile(c), q)
+            wait = functools.partial(arrivals, v_buf, v_recv, q, False, True, own)
+            acc = combine_as_they_come(v_buf, tile(c), q, wait, 0)
             f_buf[q, r] = pack(acc)
             if is_last:
                 far_first(lambda row: to_row(f_buf.at[q, r], f_buf, f_send, f_recv, q, row, c).start(), False, True, False)
@@ -356,8 +365,8 @@
         nxt = c + step
 
         def one(q):
-            gather(buf, recv, q, step > 0)
-            acc = combine(buf, tile(nxt), q)
+            wait = functools.partial(gather, buf, recv, q, step > 0)
+            acc = combine_as_they_come(buf, tile(nxt), q, wait, n_row - 1 if step > 0 else 0)
             wait_run(run_in, run_recv, nxt, q)
             stage[q] = run_in[nxt, q] - pack(acc)
             far_first(
@@ -384,8 +393,8 @@
 
     def backward_of(buf, recv, own, is_first):
         def one(q):
-            arrivals(buf, recv, q, True, False, own)
-            acc = combine(buf, upper, q)
+            wait = functools.partial(arrivals, buf, recv, q, True, False, own)
+            acc = combine_as_they_come(buf, upper, q, wait, n_row - 1)
             if not is_first:
                 s_buf[q, r] = pack(acc)
                 spread(lambda row: to_row(s_buf.at[q, r], s_buf, s_send, s_recv, q, row, c).start(), False)
@@ -520,6 +529,14 @@
         ],
         compiler_params=pltpu.CompilerParams(collective_id=0, has_side_effects=True, vmem_limit_bytes=60 << 20),
     )(factors, right_side.transpose(0, 2, 1))
+
+    def keep(forward_ref, backward_ref, forward_out, backward_out):
+        forward_out[...] = forward_ref[...]
+        backward_out[...] = backward_ref[...]
+
+    forward, backward = pl.pallas_call(
+        keep, out_shape=(shape, shape), in_specs=[vmem, vmem], out_specs=(vmem, vmem)
+    )(forward, backward)
     return forward.transpose(0, 2, 1), backward.transpose(0, 2, 1)
 
 

time: 88.2 us -> 85.2 us (0.966)
  local copies, waits for them, and re-layouts: 3.16 us -> 0 us
    unnamed x2 -> x0, local copies, waits for them, and re-layouts: 3.16 us -> none
    pallas_call x0 -> x1, Pallas kernels: none -> 1.7 us  [local(): pl.pallas_call(keep, out_shape=(shape, shape), in_specs=[vmem, vmem], out...]
    pallas_call x1, Pallas kernels: 84.2 us -> 82.7 us  [local(): pl.pallas_call(functools.partial(kernel, n_row, n_col, chunks, rows, size...]
where the time goes in v4:
time: 85.2 us; the launch traced here: 85 us
  Pallas kernels  84.4 us (99%)
    pallas_call x1, Pallas kernels, local(): pl.pallas_call(functools.partial(kernel, n_row, n_col, chunks, rows, size...  82.7 us

profile of v4, /device:TPU:0, one launch (start us, length us, event | category | flops | bytes accessed | tf_op | source)
XLA Modules:
  0.0 85.0 jit_solution(3813106702234808991)
XLA Ops:
  0.6 82.7 %shard_map.41 = (f32[1,96,320]{2,1,0:T(8,128)}, f32[1,96,320]{2,1,0:T(8,128)}) custom-call(f32[4,320,1280]{2,1,0:T(8,128)} %factors_hbm.1, f32[1,96,320]{2,1,0:T(8,128)} %bitcast.3), custom_call_target="tpu_custom_call" | custom-call | tf_op jit(solution)/shard_map/pallas_call | solution.py:516
  83.3 1.7 %shard_map.42 = (f32[1,96,320]{2,1,0:T(8,128)}, f32[1,96,320]{2,1,0:T(8,128)}) custom-call(f32[1,96,320]{2,1,0:T(8,128)} %get-tuple-element.6.forward_ref, f32[1,96,320]{2,1,0:T(8,128)} %get-tuple-element.7.backward_ref), custom_call_target="tpu_custom_call" | custom-call | tf_op jit(solution)/shard_map/pallas_call | solution.py:537

commit v5 on v4

--- a/solution.py
+++ b/solution.py
@@ -419,6 +419,45 @@
     down, down_rest = sweep_of(f_buf, f_recv, last - c, 1, rin, r_recv, rout, r_send, t_buf, v_buf, w_send, v_recv)
     back, back_rest = sweep_of(s_buf, s_recv, c, -1, rbin, rb_recv, rbout, rb_send, tb_buf, w_buf, v_send, w_recv)
 
+    def sent(src, send):
+        remote(src, src, send, send, r, c).wait_send()
+
+    def finish(q):
+        @pl.when(c == 0)
+        def _():
+            far_first(lambda row: sent(rs_buf.at[q], v_send.at[q, row]), True, False, False)
+
+        @pl.when(c > 0)
+        def _():
+            sent(rs_buf.at[q], r_send.at[c, q])
+            far_first(lambda row: sent(tb_buf.at[q], v_send.at[q, row]), False, True, True)
+            spread(lambda row: sent(s_buf.at[q, r], s_send.at[q, row]), False)
+            relayed(lambda s, row, slot: sent(s_buf.at[q, s], g_send.at[q, s, slot]), False)
+
+        @pl.when(c < last)
+        def _():
+            spread(lambda row: sent(f_buf.at[q, r], f_send.at[q, row]), True)
+            relayed(lambda s, row, slot: sent(f_buf.at[q, s], g_send.at[q, s, slot]), True)
+            sent(f_buf.at[q, r], b0_send.at[q])
+            far_first(lambda row: sent(t_buf.at[q], w_send.at[q, row]), True, False, True)
+
+        @pl.when(c == last)
+        def _():
+            far_first(lambda row: sent(f_buf.at[q, r], f_send.at[q, row]), False, True, False)
+
+        def run(k, _):
+            @pl.when(k > c + 1)
+            def _():
+                sent(rout.at[k, q], r_send.at[k, q])
+
+            @pl.when(k < c - 1)
+            def _():
+                sent(rbout.at[k, q], rb_send.at[k, q])
+
+            return 0
+
+        lax.fori_loop(0, n_col, run, 0)
+
     pass_down = pass_on_of(f_buf, f_recv, True)
     pass_back = pass_on_of(s_buf, s_recv, False)
 
@@ -431,8 +470,8 @@
 
         pipeline(
             4 * last + 1,
-            (1, pass_down), (1, down), (0, forward_of(False, False)), (DELAY - 1, enter_next), (1, down_rest),
-            (4 * last + 1, backward_of(w_buf, w_recv, True, True)),
+            (1, pass_down), (1, down), (0, forward_of(False, False)), (0, enter_next), (1, down_rest),
+            (4 * last, finish), (4 * last + 1, backward_of(w_buf, w_recv, True, True)),
         )
 
     @pl.when((c > 0) & (c < last))
@@ -453,46 +492,9 @@
             (2, back_rest),
         )
 
-    def sent(src, send):
-        remote(src, src, send, send, r, c).wait_send()
-
-    def finish(q):
-        @pl.when(c == 0)
-        def _():
-            far_first(lambda row: sent(rs_buf.at[q], v_send.at[q, row]), True, False, False)
-
-        @pl.when(c > 0)
-        def _():
-            sent(rs_buf.at[q], r_send.at[c, q])
-            far_first(lambda row: sent(tb_buf.at[q], v_send.at[q, row]), False, True, True)
-            spread(lambda row: sent(s_buf.at[q, r], s_send.at[q, row]), False)
-            relayed(lambda s, row, slot: sent(s_buf.at[q, s], g_send.at[q, s, slot]), False)
-
-        @pl.when(c < last)
-        def _():
-            spread(lambda row: sent(f_buf.at[q, r], f_send.at[q, row]), True)
-            relayed(lambda s, row, slot: sent(f_buf.at[q, s], g_send.at[q, s, slot]), True)
-            sent(f_buf.at[q, r], b0_send.at[q])
-            far_first(lambda row: sent(t_buf.at[q], w_send.at[q, row]), True, False, True)
-
-        @pl.when(c == last)
-        def _():
-            far_first(lambda row: sent(f_buf.at[q, r], f_send.at[q, row]), False, True, False)
-
-        def run(k, _):
-            @pl.when(k > c + 1)
-            def _():
-                sent(rout.at[k, q], r_send.at[k, q])
-
-            @pl.when(k < c - 1)
-            def _():
-                sent(rbout.at[k, q], rb_send.at[k, q])
-
-            return 0
-
-        lax.fori_loop(0, n_col, run, 0)
-
-    each_chunk(finish)
+    @pl.when(c > 0)
+    def _():
+        each_chunk(finish)
 
 
 def local(n_row, n_col, factors, right_side):

time: 85.2 us -> 83.1 us (0.975)
  Pallas kernels: 84.4 us -> 82.3 us
    pallas_call x1, Pallas kernels: 82.7 us -> 80.6 us  [local(): pl.pallas_call(functools.partial(kernel, n_row, n_col, chunks, rows, size...]
where the time goes in v5:
time: 83.1 us; the launch traced here: 82.9 us
  Pallas kernels  82.3 us (99%)
    pallas_call x1, Pallas kernels, local(): pl.pallas_call(functools.partial(kernel, n_row, n_col, chunks, rows, size...  80.6 us
    pallas_call x1, Pallas kernels, local(): pl.pallas_call(keep, out_shape=(shape, shape), in_specs=[vmem, vmem], out...  1.7 us

profile of v5, /device:TPU:0, one launch (start us, length us, event | category | flops | bytes accessed | tf_op | source)
XLA Modules:
  0.0 82.9 jit_solution(6128157869416224874)
XLA Ops:
  0.6 80.6 %shard_map.41 = (f32[1,96,320]{2,1,0:T(8,128)}, f32[1,96,320]{2,1,0:T(8,128)}) custom-call(f32[4,320,1280]{2,1,0:T(8,128)} %factors_hbm.1, f32[1,96,320]{2,1,0:T(8,128)} %bitcast.3), custom_call_target="tpu_custom_call" | custom-call | tf_op jit(solution)/shard_map/pallas_call | solution.py:518
  81.2 1.7 %shard_map.42 = (f32[1,96,320]{2,1,0:T(8,128)}, f32[1,96,320]{2,1,0:T(8,128)}) custom-call(f32[1,96,320]{2,1,0:T(8,128)} %get-tuple-element.6.forward_ref, f32[1,96,320]{2,1,0:T(8,128)} %get-tuple-element.7.backward_ref), custom_call_target="tpu_custom_call" | custom-call | tf_op jit(solution)/shard_map/pallas_call | solution.py:539
